TPU v7x, 256 devices: a 4x2x16 block of a 4x16x16 slice. The times are simulated.
256 devices in a mesh: pb: 2 (over y), col: 32 (over z, core), row: 4 (over x).
Axes of the slice: x: 4, y: 2, z: 16, core: 2. Of those that a mesh axis runs over, the one named last changes fastest.
The devices are a block of a 4x16x16 slice.
Arguments:
- pair_density: bfloat16 [6144, 6144], P(('pb', 'col'), 'row'), parts along dimension 0, may hold values from -0.19921875 to 0.19921875
- band_pairs: int32 [2, 3072], replicated, may hold values from 0 to 255, as said below
- valence: float32 [256], replicated, may hold values from -12 to -2
- conduction: float32 [12], replicated, may hold values from 1 to 8
- wave_vectors: int32 [3, 12288], P(None, 'pb'), parts along dimension 1, may hold values from -6 to 6
- momentum: float32 [6], P('pb'), parts along dimension 0, may hold values from 0.3 to 0.7
- guess_scale: float32 [12288], P('pb'), parts along dimension 0, may hold values from 0.4 to 0.75
Outputs:
- epsilon: float32 [12288, 6144], P(('pb', 'row'), 'col'), parts along dimension 0
- inverse: float32 [12288, 6144], P(('pb', 'row'), 'col'), parts along dimension 0
There are 2 independent parts, one for each index of `pb`. A program takes and returns all parts, laid end to end along the dimension named above; an argument that names none is the same for every part. Nothing has to cross between parts.
Inputs may be any that keep to these rules, and one draw needn't show every extreme that they name: `band_pairs`: column p names a valence band below 256 in row 0 and a conduction band below 12 in row 1; every such pair of bands appears in exactly one column.
All inputs are finite; a program needn't handle non-finite values.
Results may differ from a plain program's by a relative error of at most 0.0036.
The roundings to bfloat16 on the way count: a program that leaves them out, or rounds other values in their place, can miss the bound.
Values may be sent and summed in bfloat16 or wider, within the bound.
No kernel may reach another device: no remote copies, remote signals or barrier semaphores. Data moves between devices by JAX's collectives and lax.ppermute only.
A program may use at most 64 MiB of HBM per device.

v0:
```python
import math
import jax
import jax.numpy as jnp
from jax import lax
from jax.sharding import PartitionSpec as P


def copy_for_each(array, axis):
    copies = jnp.broadcast_to(array, (lax.axis_size(axis), *array.shape))
    return lax.all_to_all(copies, axis, split_axis=0, concat_axis=0, tiled=True)


def in_order(pieces, dim):
    lengths = list(pieces.shape[1:])
    lengths[dim] *= pieces.shape[0]
    return jnp.moveaxis(pieces, 0, dim).reshape(lengths)


def gathered_copies(array, axis, dim):
    pieces = copy_for_each(array, axis)
    return in_order(pieces, dim)


def lookup(indices, table):
    levels = jnp.arange(table.shape[0], dtype=jnp.int32)
    picked = indices[:, None] == levels[None, :]
    return jnp.sum(jnp.where(picked, table[None, :], 0.0), axis=1)


def on_device(pair_density, band_pairs, valence, conduction, wave_vectors, momentum, guess_scale):
    column_index = lax.axis_index("col")
    row_index = lax.axis_index("row")
    row_height = pair_density.shape[1]
    whole_width = row_height * lax.axis_size("row")
    strip_width = whole_width // lax.axis_size("col")
    valence_of = lookup(band_pairs[0], valence)
    conduction_of = lookup(band_pairs[1], conduction)
    weight = 4.0 / (valence_of - conduction_of)
    shifted = wave_vectors.astype(jnp.float32) + momentum[:, None]
    sqrt_all = jnp.sqrt(4.0 * math.pi / jnp.sum(shifted * shifted, axis=0))
    row_first = row_index * row_height
    column_first = column_index * strip_width
    sqrt_rows = lax.dynamic_slice_in_dim(sqrt_all, row_first, row_height, 0)
    sqrt_cols = lax.dynamic_slice_in_dim(sqrt_all, column_first, strip_width, 0)
    scale_rows = lax.dynamic_slice_in_dim(guess_scale, row_first, row_height, 0)
    scale_cols = lax.dynamic_slice_in_dim(guess_scale, column_first, strip_width, 0)
    panel_pairs = lax.all_gather(pair_density, "col", axis=0, tiled=True)
    owner = column_first // row_height
    offset = column_first % row_height
    own_slice = lax.dynamic_slice_in_dim(panel_pairs, offset, strip_width, 1)
    candidates = lax.all_gather(own_slice, "row", axis=1, tiled=True)
    strip_pairs = lax.dynamic_slice_in_dim(candidates, owner * strip_width, strip_width, 1)
    weighted = (weight[:, None] * panel_pairs.astype(jnp.float32)).astype(jnp.bfloat16)
    weighted_strip = (weight[:, None] * strip_pairs.astype(jnp.float32)).astype(jnp.bfloat16)
    chi_block = lax.dot_general(
        weighted, strip_pairs, (((0,), (0,)), ((), ())), preferred_element_type=jnp.float32
    )
    chi_rows = jnp.sum(weighted.astype(jnp.float32) * panel_pairs.astype(jnp.float32), axis=0)
    chi_cols = jnp.sum(weighted_strip.astype(jnp.float32) * strip_pairs.astype(jnp.float32), axis=0)
    global_rows = row_first + jnp.arange(row_height, dtype=jnp.int32)
    global_cols = column_first + jnp.arange(strip_width, dtype=jnp.int32)
    identity = (global_rows[:, None] == global_cols[None, :]).astype(jnp.float32)
    epsilon = identity - sqrt_rows[:, None] * chi_block * sqrt_cols[None, :]
    guess_rows = scale_rows / (1.0 - sqrt_rows * chi_rows * sqrt_rows)
    guess_cols = scale_cols / (1.0 - sqrt_cols * chi_cols * sqrt_cols)
    mixed = epsilon * guess_cols[None, :]
    mixed_b = mixed.astype(jnp.bfloat16)
    panel_mixed = lax.all_gather(mixed_b, "col", axis=1, tiled=True)
    strip_mixed = gathered_copies(mixed_b, "row", 0)
    square = jnp.dot(panel_mixed, strip_mixed, preferred_element_type=jnp.float32)
    square_b = square.astype(jnp.bfloat16)
    strip_square = gathered_copies(square_b, "row", 0)
    cube = jnp.dot(panel_mixed, strip_square, preferred_element_type=jnp.float32)
    inverse = guess_rows[:, None] * (4.0 * identity - 6.0 * mixed + 4.0 * square - cube)
    return (epsilon, inverse)


def solution(mesh):
    placed = (P(("pb", "col"), "row"), P(), P(), P(), P(None, "pb"), P("pb"), P("pb"))
    return jax.shard_map(
        on_device,
        mesh=mesh,
        in_specs=placed,
        out_specs=(P(("pb", "row"), "col"), P(("pb", "row"), "col")),
        check_vma=False,
    )
```

profile of v0, /device:TPU:33, one launch (start us, length us, event | category | flops | bytes accessed | tf_op | source)
XLA Modules:
  0.0 345.0 jit_solution(10228950458131673058)
XLA Ops:
  7.2 0.1 all-gather.4.cloned.1.call-start
  7.2 0.7 all-gather.4.cloned.1.call-update
  8.0 0.1 all-gather.6.cloned.1.call-start
  8.1 94.8 %all-gather.4.cloned.1.call-done = bf16[3072,1536]{1,0:T(8,128)(2,1)} async-done(((bf16[96,1536]{1,0:T(8,128)(2,1)}), bf16[3072,1536]{1,0:T(8,128)(2,1)}) %all-gather.4.cloned.1.call-update) | async-done | bytes 9437200 | tf_op jit(solution)/shard_map/all_gather | solution.py:47
  102.8 2.4 constant_dynamic-slice_fusion
  105.3 0.0 copy-start.1
  105.3 0.0 copy-start.4
  105.3 0.0 copy-start
  105.3 0.0 copy-start.3
  105.3 0.0 copy-start.2
  105.3 1.5 copy.18
  106.8 0.1 all-gather.6.cloned.1.call-update
  106.9 0.1 all-gather.8.cloned.1.call-start
  107.0 0.0 copy-done.1
  107.0 0.0 copy-done.4
  107.0 0.1 select_reduce_fusion.1
  107.1 0.0 copy-done
  107.2 0.0 copy-done.3
  107.2 0.1 multiply_reduce_fusion
  107.3 0.0 copy-done.2
  107.3 1.9 select_reduce_fusion
  109.2 6.2 %fusion.1 = f32[1536]{0:T(1024)S(1)} fusion(bf16[3072,1536]{1,0:T(8,128)(2,1)} %all-gather.4.cloned.1.call-done, f32[3072]{0:T(1024)S(1)} %subtract_divide_fusion), kind=kLoop, calls=%fused_computation.3 | loop fusion | flops 28310016 | bytes 9455616 | tf_op jit(solution)/shard_map/reduce_sum | solution.py:58
  115.5 0.8 fusion.20
  116.3 44.8 %all-gather.6.cloned.1.call-done = bf16[3072,768]{0,1:T(8,128)(2,1)} async-done(((bf16[3072,192]{0,1:T(8,128)(2,1)}), bf16[3072,768]{0,1:T(8,128)(2,1)}) %all-gather.6.cloned.1.call-update) | async-done | bytes 4718608 | tf_op jit(solution)/shard_map/all_gather | solution.py:51
  161.0 1.7 fusion.15
  162.7 0.8 fusion.22
  163.5 7.6 %multiply_convert_fusion = (bf16[1536,192]{0,1:T(8,128)(2,1)}, f32[1536,192]{0,1:T(8,128)}) fusion(f32[192]{0:T(256)S(1)} %get-tuple-element.4, f32[192]{0:T(256)S(1)} %get-tuple-element.5, bf16[3072,1536]{1,0:T(8,128)(2,1)} %all-gather.4.cloned.1.call-done, f32[3072]{0:T(1024)S(1)} %subtract_divide_fusion, ...), kind=kOutput, calls=%fused_computation.20 | convolution fusion | flops 1828159488 | bytes 12413188 | tf_op jit(solution)/shard_map/dot_general | solution.py:55
  171.1 0.1 all-gather.8.cloned.1.call-update
  171.2 1.2 broadcast_in_dim.47
  172.4 31.0 %all_to_all.10 = bf16[4,1536,192]{1,2,0:T(8,128)(2,1)S(1)} all-to-all(bf16[4,1536,192]{1,2,0:T(8,128)(2,1)S(1)} %broadcast_in_dim.47), channel_id=1, replica_groups=mesh['pb'=2,'col'=32,'row'=4] {'row'}, dimensions={0} | all-to-all | bytes 4718592 | tf_op jit(solution)/shard_map/all_to_all | solution.py:10
  203.5 0.3 copy.21
  203.7 84.0 %all-gather.8.cloned.1.call-done = bf16[1536,6144]{0,1:T(8,128)(2,1)} async-done(((bf16[1536,192]{0,1:T(8,128)(2,1)}), bf16[1536,6144]{0,1:T(8,128)(2,1)}) %all-gather.8.cloned.1.call-update) | async-done | bytes 18874384 | tf_op jit(solution)/shard_map/all_gather | solution.py:68
  287.8 0.0 slice-start
  287.8 0.0 slice-start.1
  287.8 0.0 slice-start.2
  287.8 11.4 %fusion.25 = (bf16[1536,192]{0,1:T(8,128)(2,1)S(1)}, f32[1536,192]{0,1:T(8,128)}) fusion(bf16[6144,192]{0,1:T(8,128)(2,1)S(1)} %bitcast.13, bf16[1536,6144]{0,1:T(8,128)(2,1)} %all-gather.8.cloned.1.call-done), kind=kOutput, calls=%fused_computation.38 | convolution fusion | flops 3624173568 | bytes 23003136 | tf_op jit(solution)/shard_map/dot_general | solution.py:70
  299.1 0.2 broadcast_in_dim.48
  299.3 0.0 slice-start.4
  299.3 32.6 %all_to_all.11 = bf16[4,1536,192]{1,2,0:T(8,128)(2,1)S(1)} all-to-all(bf16[4,1536,192]{1,2,0:T(8,128)(2,1)S(1)} %broadcast_in_dim.48), channel_id=1, replica_groups=mesh['pb'=2,'col'=32,'row'=4] {'row'}, dimensions={0} | all-to-all | bytes 4718592 | tf_op jit(solution)/shard_map/all_to_all | solution.py:10
  331.9 0.3 copy.22
  332.2 0.0 slice-done
  332.2 0.0 slice-done.1
  332.2 0.0 slice-done.2
  332.2 0.0 slice-done.3
  332.2 0.0 slice-done.4
  332.2 1.0 copy-done.5
  333.2 0.4 copy-done.6
  333.6 4.9 %fusion.13 = f32[1536,192]{0,1:T(8,128)} fusion(bf16[6144,192]{0,1:T(8,128)(2,1)S(1)} %bitcast.12, bf16[1536,6144]{0,1:T(8,128)(2,1)S(1)} %bitcast.17, f32[1536,192]{0,1:T(8,128)S(1)} %copy-done.6, f32[1536,192]{0,1:T(8,128)S(1)} %copy-done.5, f32[192]{0:T(256)S(1)} %get-tuple-element.4, f32[1536]{0:T(1024)S(1)} %get-tuple-element.2, ...), kind=kOutput, calls=%fused_computation.13 | convolution fusion | flops 3626532864 | bytes 24786432 | tf_op jit(solution)/shard_map/dot_general | solution.py:73
  (9 shorter events, 0.1 us)
Async XLA Ops:
  7.2 95.7 %all-gather.4.cloned.1.call-start = ((), (), s32[]{:S(2)}) async-start(), calls=%async_computation.2 | async-start | bytes 9732096 | tf_op jit(solution)/shard_map/all_gather | solution.py:47
  8.0 153.0 %all-gather.6.cloned.1.call-start = ((), (), s32[]{:S(2)}) async-start(), calls=%async_computation.3 | async-start | bytes 5898240 | tf_op jit(solution)/shard_map/all_gather | solution.py:51
  105.3 1.7 copy-start.1
  105.3 1.7 copy-start.4
  105.3 1.9 copy-start
  105.3 1.9 copy-start.3
  105.3 2.0 copy-start.2
  106.9 180.9 %all-gather.8.cloned.1.call-start = ((), (), s32[]{:S(2)}) async-start(), calls=%async_computation.4 | async-start | bytes 19464192 | tf_op jit(solution)/shard_map/all_gather | solution.py:68
  287.8 44.4 %slice-start = ((s8[18874368]{0:T(1024)(128)(4,1)}), s8[4194304]{0:T(1024)(128)(4,1)S(1)}, s32[]{:S(2)}) async-start(s8[18874368]{0:T(1024)(128)(4,1)} %bitcast.16), calls=%async_computation.5 | async-start | bytes 8388608
  287.8 44.4 %slice-start.1 = ((s8[18874368]{0:T(1024)(128)(4,1)}), s8[4194304]{0:T(1024)(128)(4,1)S(1)}, s32[]{:S(2)}) async-start(s8[18874368]{0:T(1024)(128)(4,1)} %bitcast.16), calls=%async_computation.6 | async-start | bytes 8388608
  287.8 44.5 %slice-start.2 = ((s8[18874368]{0:T(1024)(128)(4,1)}), s8[4194304]{0:T(1024)(128)(4,1)S(1)}, s32[]{:S(2)}) async-start(s8[18874368]{0:T(1024)(128)(4,1)} %bitcast.16), calls=%async_computation.7 | async-start | bytes 8388608
  287.8 44.5 %slice-start.3 = ((s8[18874368]{0:T(1024)(128)(4,1)}), s8[4194304]{0:T(1024)(128)(4,1)S(1)}, s32[]{:S(2)}) async-start(s8[18874368]{0:T(1024)(128)(4,1)} %bitcast.16), calls=%async_computation.8 | async-start | bytes 8388608
  299.3 32.9 %slice-start.4 = ((s8[18874368]{0:T(1024)(128)(4,1)}), s8[2097152]{0:T(1024)(128)(4,1)S(1)}, s32[]{:S(2)}) async-start(s8[18874368]{0:T(1024)(128)(4,1)} %bitcast.16), calls=%async_computation.9 | async-start | bytes 4194304
  331.9 1.3 copy-start.5
  331.9 1.6 copy-start.6
Sparse Core Ops, SparseCore 0:
  9.9 92.9 all-gather.3
  107.0 53.9 all-gather.5
  171.3 116.4 all-gather.7
where the time goes:
time: 346 us; the launch traced here: 345 us
  waiting for transfers between devices  224 us (65%)
  blocking collectives  63.7 us (18%)
  matrix products  23.9 us (7%)
  between operations  14.1 us (4%)
  other arithmetic  11.6 us (3%)
  local copies, waits for them, and re-layouts  7.24 us (2%)
    all_gather x1, waiting for transfers between devices, on_device(): panel_pairs = lax.all_gather(pair_density, 'col', axis=0, tiled=True)  94.8 us
    all_gather x1, waiting for transfers between devices, on_device(): panel_mixed = lax.all_gather(mixed_b, 'col', axis=1, tiled=True)  84 us
    all_to_all x2, blocking collectives, copy_for_each(): return lax.all_to_all(copies, axis, split_axis=0, concat_axis=0, tiled=True)  63.7 us
    all_gather x1, waiting for transfers between devices, on_device(): candidates = lax.all_gather(own_slice, 'row', axis=1, tiled=True)  44.8 us
    dot_general x1, matrix products, on_device(): jnp.dot(panel_mixed, strip_mixed, preferred_element_type=jnp.float32)  11.4 us
    dot_general x1, matrix products, on_device(): lax.dot_general(weighted, strip_pairs, (((0,), (0,)), ((), ())), preferre...  7.63 us
  transfers between devices with their start and end apart: 3, of which 3 were waited for; matrix products, arithmetic and copies ran while one was open for 3% of the time, Pallas kernels for 0%

commit v1 on v0

--- a/solution.py
+++ b/solution.py
@@ -44,7 +44,9 @@
     sqrt_cols = lax.dynamic_slice_in_dim(sqrt_all, column_first, strip_width, 0)
     scale_rows = lax.dynamic_slice_in_dim(guess_scale, row_first, row_height, 0)
     scale_cols = lax.dynamic_slice_in_dim(guess_scale, column_first, strip_width, 0)
-    panel_pairs = lax.all_gather(pair_density, "col", axis=0, tiled=True)
+    panel_pairs = jnp.concatenate(
+        lax.all_to_all(jnp.stack([pair_density] * lax.axis_size("col")), "col", 0, 0), axis=0
+    )
     owner = column_first // row_height
     offset = column_first % row_height
     own_slice = lax.dynamic_slice_in_dim(panel_pairs, offset, strip_width, 1)

time: 346 us -> 694 us (2.01)
  waiting for transfers between devices: 224 us -> 541 us
  starting transfers between devices: 0.19 us -> 25.6 us
    all_to_all x0 -> x1, waiting for transfers between devices: none -> 403 us  [on_device(): lax.all_to_all(jnp.stack([pair_density] * lax.axis_size('col')), 'col', 0...]
    all_gather x1 -> x0, waiting for transfers between devices: 94.8 us -> none  [on_device(): panel_pairs = lax.all_gather(pair_density, 'col', axis=0, tiled=True)]
    all_to_all x0 -> x1, starting transfers between devices: none -> 25.5 us  [on_device(): lax.all_to_all(jnp.stack([pair_density] * lax.axis_size('col')), 'col', 0...]
    all_gather x1, waiting for transfers between devices: 44.8 us -> 53.6 us  [on_device(): candidates = lax.all_gather(own_slice, 'row', axis=1, tiled=True)]
  transfers between devices with their start and end apart: 3 -> 3, of which waited for: 3 -> 3; matrix products, arithmetic and copies ran while one was open for 3% -> 2% of each run, Pallas kernels for 0% -> 0%
where the time goes in v1:
time: 694 us; the launch traced here: 693 us
  waiting for transfers between devices  541 us (78%)
  blocking collectives  63.7 us (9%)
  starting transfers between devices  25.6 us (4%)
  matrix products  23.9 us (3%)
  between operations  14.3 us (2%)
  local copies, waits for them, and re-layouts  13 us (2%)
  other arithmetic  11.6 us (2%)
    all_to_all x1, waiting for transfers between devices, on_device(): lax.all_to_all(jnp.stack([pair_density] * lax.axis_size('col')), 'col', 0...  403 us
    all_gather x1, waiting for transfers between devices, on_device(): panel_mixed = lax.all_gather(mixed_b, 'col', axis=1, tiled=True)  84 us
    all_to_all x2, blocking collectives, copy_for_each(): return lax.all_to_all(copies, axis, split_axis=0, concat_axis=0, tiled=True)  63.7 us
    all_gather x1, waiting for transfers between devices, on_device(): candidates = lax.all_gather(own_slice, 'row', axis=1, tiled=True)  53.6 us
    all_to_all x1, starting transfers between devices, on_device(): lax.all_to_all(jnp.stack([pair_density] * lax.axis_size('col')), 'col', 0...  25.5 us
  transfers between devices with their start and end apart: 3, of which 3 were waited for; matrix products, arithmetic and copies ran while one was open for 2% of the time, Pallas kernels for 0%

profile of v1, /device:TPU:33, one launch (start us, length us, event | category | flops | bytes accessed | tf_op | source)
XLA Modules:
  0.0 693.0 jit_solution(7609673548336638979)
XLA Ops:
  7.2 5.7 stack.2
  12.9 25.5 %all-to-all-start = ((bf16[32,96,1536]{2,1,0:T(8,128)(2,1)}), bf16[32,96,1536]{2,1,0:T(8,128)(2,1)}, u32[]{:S(2)}, u32[]{:S(2)}) async-start(bf16[32,96,1536]{2,1,0:T(8,128)(2,1)} %stack.2), calls=%async_computation | async-start | bytes 18874368 | tf_op jit(solution)/shard_map/all_to_all | solution.py:48
  38.3 0.1 all-gather.3.cloned.1.call-start
  38.4 403.2 %all-to-all-done = bf16[32,96,1536]{2,1,0:T(8,128)(2,1)} async-done(((bf16[32,96,1536]{2,1,0:T(8,128)(2,1)}), bf16[32,96,1536]{2,1,0:T(8,128)(2,1)}, u32[]{:S(2)}, u32[]{:S(2)}) %all-to-all-start) | async-done | bytes 9437216 | tf_op jit(solution)/shard_map/all_to_all | solution.py:48
  441.6 2.4 constant_dynamic-slice_fusion
  444.0 0.0 copy-start.1
  444.0 0.0 copy-start.4
  444.0 0.0 copy-start.2
  444.1 0.0 copy-start
  444.1 0.0 copy-start.3
  444.1 1.5 copy.15
  445.6 0.1 all-gather.3.cloned.1.call-update
  445.6 0.1 all-gather.5.cloned.1.call-start
  445.7 0.0 copy-done.1
  445.8 0.0 copy-done.4
  445.8 0.1 select_reduce_fusion.1
  445.9 0.0 copy-done.2
  445.9 1.9 select_reduce_fusion
  447.8 0.1 div.35
  447.9 0.0 copy-done
  447.9 0.0 copy-done.3
  447.9 0.1 multiply_reduce_fusion
  448.1 6.2 fusion.1
  454.3 0.8 fusion.14
  455.1 53.6 %all-gather.3.cloned.1.call-done = bf16[3072,768]{0,1:T(8,128)(2,1)} async-done(((bf16[3072,192]{0,1:T(8,128)(2,1)}), bf16[3072,768]{0,1:T(8,128)(2,1)}) %all-gather.3.cloned.1.call-update) | async-done | bytes 4718608 | tf_op jit(solution)/shard_map/all_gather | solution.py:53
  508.7 1.7 fusion.9
  510.3 0.8 fusion.16
  511.1 7.7 %multiply_convert_fusion.8 = (bf16[1536,192]{0,1:T(8,128)(2,1)}, f32[1536,192]{0,1:T(8,128)}) fusion(f32[192]{0:T(256)S(1)} %get-tuple-element.4, f32[192]{0:T(256)S(1)} %get-tuple-element.5, bf16[3072,1536]{1,0:T(8,128)(2,1)} %bitcast.2, f32[3072]{0:T(1024)S(1)} %subtract_divide_fusion, bf16[3072,768]{0,1:T(8,128)(2,1)} %all-gather.3.cloned.1.call-done, ...), kind=kOutput, calls=%fused_computation.22 | convolution fusion | flops 1828159488 | bytes 12413188 | tf_op jit(solution)/shard_map/dot_general | solution.py:57
  518.8 0.1 all-gather.5.cloned.1.call-update
  518.8 1.2 broadcast_in_dim.47
  520.1 31.1 %all_to_all.15 = bf16[4,1536,192]{1,2,0:T(8,128)(2,1)S(1)} all-to-all(bf16[4,1536,192]{1,2,0:T(8,128)(2,1)S(1)} %broadcast_in_dim.47), channel_id=1, replica_groups=mesh['pb'=2,'col'=32,'row'=4] {'row'}, dimensions={0} | all-to-all | bytes 4718592 | tf_op jit(solution)/shard_map/all_to_all | solution.py:10
  551.2 0.3 copy.18
  551.4 84.0 %all-gather.5.cloned.1.call-done = bf16[1536,6144]{0,1:T(8,128)(2,1)} async-done(((bf16[1536,192]{0,1:T(8,128)(2,1)}), bf16[1536,6144]{0,1:T(8,128)(2,1)}) %all-gather.5.cloned.1.call-update) | async-done | bytes 18874384 | tf_op jit(solution)/shard_map/all_gather | solution.py:70
  635.4 0.0 slice-start
  635.4 0.0 slice-start.1
  635.4 11.4 %fusion.19 = (bf16[1536,192]{0,1:T(8,128)(2,1)S(1)}, f32[1536,192]{0,1:T(8,128)}) fusion(bf16[6144,192]{0,1:T(8,128)(2,1)S(1)} %bitcast.14, bf16[1536,6144]{0,1:T(8,128)(2,1)} %all-gather.5.cloned.1.call-done), kind=kOutput, calls=%fused_computation.40 | convolution fusion | flops 3624173568 | bytes 23003136 | tf_op jit(solution)/shard_map/dot_general | solution.py:72
  646.8 0.2 broadcast_in_dim.48
  647.0 0.0 slice-start.4
  647.0 32.6 %all_to_all.16 = bf16[4,1536,192]{1,2,0:T(8,128)(2,1)S(1)} all-to-all(bf16[4,1536,192]{1,2,0:T(8,128)(2,1)S(1)} %broadcast_in_dim.48), channel_id=1, replica_groups=mesh['pb'=2,'col'=32,'row'=4] {'row'}, dimensions={0} | all-to-all | bytes 4718592 | tf_op jit(solution)/shard_map/all_to_all | solution.py:10
  679.6 0.3 copy.19
  679.8 0.0 slice-done
  679.8 0.0 slice-done.1
  679.9 0.0 slice-done.2
  679.9 0.0 slice-done.3
  679.9 0.0 slice-done.4
  679.9 1.0 copy-done.5
  680.8 0.4 copy-done.6
  681.2 4.9 fusion.7
  (10 shorter events, 0.1 us)
Async XLA Ops:
  12.9 428.7 %all-to-all-start = ((bf16[32,96,1536]{2,1,0:T(8,128)(2,1)}), bf16[32,96,1536]{2,1,0:T(8,128)(2,1)}, u32[]{:S(2)}, u32[]{:S(2)}) async-start(bf16[32,96,1536]{2,1,0:T(8,128)(2,1)} %stack.2), calls=%async_computation | async-start | bytes 18874368 | tf_op jit(solution)/shard_map/all_to_all | solution.py:48
  38.3 470.3 %all-gather.3.cloned.1.call-start = ((), (), s32[]{:S(2)}) async-start(), calls=%async_computation.3 | async-start | bytes 5898240 | tf_op jit(solution)/shard_map/all_gather | solution.py:53
  444.0 1.7 copy-start.1
  444.0 1.7 copy-start.4
  444.0 1.8 copy-start.2
  444.1 3.8 copy-start
  444.1 3.8 copy-start.3
  445.6 189.8 %all-gather.5.cloned.1.call-start = ((), (), s32[]{:S(2)}) async-start(), calls=%async_computation.4 | async-start | bytes 19464192 | tf_op jit(solution)/shard_map/all_gather | solution.py:70
  635.4 44.4 %slice-start = ((s8[18874368]{0:T(1024)(128)(4,1)}), s8[4194304]{0:T(1024)(128)(4,1)S(1)}, s32[]{:S(2)}) async-start(s8[18874368]{0:T(1024)(128)(4,1)} %bitcast.17), calls=%async_computation.5 | async-start | bytes 8388608
  635.4 44.4 %slice-start.1 = ((s8[18874368]{0:T(1024)(128)(4,1)}), s8[4194304]{0:T(1024)(128)(4,1)S(1)}, s32[]{:S(2)}) async-start(s8[18874368]{0:T(1024)(128)(4,1)} %bitcast.17), calls=%async_computation.6 | async-start | bytes 8388608
  635.4 44.5 %slice-start.2 = ((s8[18874368]{0:T(1024)(128)(4,1)}), s8[4194304]{0:T(1024)(128)(4,1)S(1)}, s32[]{:S(2)}) async-start(s8[18874368]{0:T(1024)(128)(4,1)} %bitcast.17), calls=%async_computation.7 | async-start | bytes 8388608
  635.4 44.5 %slice-start.3 = ((s8[18874368]{0:T(1024)(128)(4,1)}), s8[4194304]{0:T(1024)(128)(4,1)S(1)}, s32[]{:S(2)}) async-start(s8[18874368]{0:T(1024)(128)(4,1)} %bitcast.17), calls=%async_computation.8 | async-start | bytes 8388608
  647.0 32.9 %slice-start.4 = ((s8[18874368]{0:T(1024)(128)(4,1)}), s8[2097152]{0:T(1024)(128)(4,1)S(1)}, s32[]{:S(2)}) async-start(s8[18874368]{0:T(1024)(128)(4,1)} %bitcast.17), calls=%async_computation.9 | async-start | bytes 4194304
  679.6 1.3 copy-start.5
  679.6 1.6 copy-start.6
Sparse Core Ops, SparseCore 0:
  445.7 62.8 all-gather.2
  518.9 116.4 all-gather.4
